TPU v7x, 128 devices: a whole 4x4x4 slice. The times are simulated.
128 devices in a mesh: vocab: 64 (over y, x, z), batch: 2 (over core).
Axes of the slice: x: 4, y: 4, z: 4, core: 2. Of those that a mesh axis runs over, the one named last changes fastest.
Arguments:
- hidden: bfloat16 [2048, 7168], P(('batch', 'vocab')), parts along dimension 0, may hold values from -1000 to 1000
- norm_gain: bfloat16 [7168], replicated, may hold values from 1.5 to 5
- lm_head: bfloat16 [7168, 65536], P(None, 'vocab'), may hold values from -2 to 2
- draft_logits: bfloat16 [2048, 65536], P('batch', 'vocab'), parts along dimension 0, may hold values from -480 to 480
- draft_tokens: int32 [2048], P('batch'), parts along dimension 0, may hold values from 0 to 65535
- tree_parents: int32 [2048], P('batch'), parts along dimension 0, may hold values from 0 to 62, as said below
- node_depths: int32 [2048], P('batch'), parts along dimension 0, may hold values from 0 to 8, as said below
- uniforms: float32 [2048], P('batch'), parts along dimension 0, may hold values from 0 to 1
Outputs:
- target_lse: float32 [2048], P('batch'), parts along dimension 0
- token_logprob: float32 [2048], P('batch'), parts along dimension 0
- residual_mass: float32 [2048], P('batch'), parts along dimension 0
- accept_margin: float32 [2048], P('batch'), parts along dimension 0
- path_margin: float32 [2048], P('batch'), parts along dimension 0
There are 2 independent parts, one for each index of `batch`. A program takes and returns all parts, laid end to end along the dimension named above; an argument that names none is the same for every part. Nothing has to cross between parts.
Inputs may be any that keep to these rules, and one draw needn't show every extreme that they name: `tree_parents`: rows come in 16 requests of 64 consecutive rows, the first of each being the root. A node's entry is the position of its parent within the request, smaller than its own position; the root's entry is 0. `node_depths`: A node's depth is its parent's depth plus one, the root's is 0; in every request some node has depth 8.
All inputs are finite; a program needn't handle non-finite values.
Results may differ from a plain program's by a relative error of at most 0.0049.
Values may be sent and summed in bfloat16 or wider, within the bound.
A program may use at most 128 MiB of HBM per device.

v0:
```python
import jax
import jax.numpy as jnp
from jax import lax
from jax.sharding import PartitionSpec as P

NODES = 64
DEPTH_MAX = 8


epsilon = 1e-06
highest = lax.Precision.HIGHEST


def sent_to_all(x, axis):
    copies = jnp.broadcast_to(x, (lax.axis_size(axis), *x.shape))
    return lax.all_to_all(copies, axis, split_axis=0, concat_axis=0, tiled=True)


def collected_together(x, axis):
    leaves = jax.tree.leaves(x)
    order = sorted(range(len(leaves)), key=lambda k: -leaves[k].size)
    width = (1, *leaves[order[0]].shape)[-1]
    lines = [
        jnp.pad(leaves[k].reshape(-1), (0, -leaves[k].size % width)).reshape(-1, width)
        for k in order
    ]
    both, at, found = (sent_to_all(jnp.concatenate(lines), axis), 0, {})
    for k, line in zip(order, lines):
        share = both[:, at : at + len(line)].reshape(len(both), -1)
        found[k] = share[:, : leaves[k].size].reshape(-1, *leaves[k].shape)
        at += len(line)
    numbers = iter(range(len(leaves)))
    return jax.tree.map(lambda _: found[next(numbers)], x)


def joined_by_halves(pieces, combine):
    while len(jax.tree.leaves(pieces)[0]) > 1:
        pieces = jax.vmap(combine)(
            *(jax.tree.map(lambda part: part[side::2], pieces) for side in (0, 1))
        )
    return jax.tree.map(lambda part: part[0], pieces)


def combined_all(x, axis, combine):
    pieces = collected_together(x, axis)
    return joined_by_halves(pieces, combine)


def taken_together(x, axis):
    return sent_to_all(x, axis).sum(axis=0)


def together(arrays, axis):
    ends = [0]
    for a in arrays:
        ends.append(ends[-1] + a.size)
    total = taken_together(jnp.concatenate([a.ravel() for a in arrays]), axis)
    return tuple((total[b:e].reshape(a.shape) for a, b, e in zip(arrays, ends, ends[1:])))


def normalize(hidden_rows, gain_vector):
    values = hidden_rows.astype(jnp.float32)
    mean_square = jnp.mean(values * values, axis=1, keepdims=True)
    scaled = values * lax.rsqrt(mean_square + epsilon) * gain_vector.astype(jnp.float32)
    return scaled.astype(jnp.bfloat16)


def join_stats(left_part, right_part):
    target_max = jnp.maximum(left_part[0], right_part[0])
    target_sum = left_part[1] * jnp.exp(left_part[0] - target_max) + right_part[1] * jnp.exp(
        right_part[0] - target_max
    )
    draft_max = jnp.maximum(left_part[2], right_part[2])
    draft_sum = left_part[3] * jnp.exp(left_part[2] - draft_max) + right_part[3] * jnp.exp(
        right_part[2] - draft_max
    )
    return (target_max, target_sum, draft_max, draft_sum)


def body(
    hidden, norm_gain, lm_head, draft_logits, draft_tokens, tree_parents, node_depths, uniforms
):
    vocab_dev = lm_head.shape[1]
    rows_all = draft_tokens.shape[0]
    requests = rows_all // NODES
    offset = lax.axis_index("vocab") * vocab_dev
    normed = normalize(hidden, norm_gain)
    local_column = draft_tokens - offset
    owned_here = (local_column >= 0) & (local_column < vocab_dev)
    vocab_iota = jnp.arange(vocab_dev, dtype=jnp.int32)
    column_hot = (local_column[:, None] == vocab_iota[None, :]) & owned_here[:, None]
    column_float = column_hot.astype(jnp.float32)
    column_half = column_hot.astype(jnp.bfloat16)
    node_iota = jnp.arange(NODES, dtype=jnp.int32)
    parent_hot = (
        tree_parents.reshape(requests, NODES)[:, :, None] == node_iota[None, None, :]
    ).astype(jnp.float32)

    def at_parent(vector):
        return jnp.einsum(
            "rkn,rn->rk", parent_hot, vector.reshape(requests, NODES), precision=highest
        ).reshape(rows_all)

    logits = jnp.dot(
        lax.all_gather(normed, "vocab", axis=0, tiled=True),
        lm_head,
        preferred_element_type=jnp.float32,
    )
    draft_values = draft_logits.astype(jnp.float32)
    local_target = jnp.max(logits, axis=1)
    local_draft = jnp.max(draft_values, axis=1)
    local_terms = (
        local_target,
        jnp.sum(jnp.exp(logits - local_target[:, None]), axis=1),
        local_draft,
        jnp.sum(jnp.exp(draft_values - local_draft[:, None]), axis=1),
    )
    target_max, target_sum, draft_max, draft_sum = combined_all(local_terms, "vocab", join_stats)
    target_lse = target_max + jnp.log(target_sum)
    draft_lse = draft_max + jnp.log(draft_sum)
    excess = jnp.maximum(
        jnp.exp(logits - target_lse[:, None]) - jnp.exp(draft_values - draft_lse[:, None]), 0.0
    )
    target_cols = jnp.einsum(
        "rnv,rkv->rnk",
        logits.reshape(requests, NODES, vocab_dev),
        column_float.reshape(requests, NODES, vocab_dev),
        precision=highest,
    )
    draft_cols = jnp.einsum(
        "rnv,rkv->rnk",
        draft_logits.reshape(requests, NODES, vocab_dev),
        column_half.reshape(requests, NODES, vocab_dev),
        preferred_element_type=jnp.float32,
    )
    picked_target = jnp.einsum("rkn,rnk->rk", parent_hot, target_cols).reshape(rows_all)
    picked_draft = jnp.einsum("rkn,rnk->rk", parent_hot, draft_cols).reshape(rows_all)
    picked_target, picked_draft = (picked_target, picked_draft)
    residual, picked_target, picked_draft = together(
        (jnp.sum(excess, axis=1), picked_target, picked_draft), "vocab"
    )
    target_lse, draft_lse, residual_mass, picked_target, picked_draft = (
        target_lse,
        draft_lse,
        residual,
        picked_target,
        picked_draft,
    )
    token_logprob = picked_target - at_parent(target_lse)
    draft_logprob = picked_draft - at_parent(draft_lse)
    accept_margin = jnp.exp(jnp.minimum(token_logprob - draft_logprob, 0.0)) - uniforms
    path_margin = jnp.ones((rows_all,), jnp.float32)
    for level_now in range(1, DEPTH_MAX + 1):
        path_margin = jnp.where(
            node_depths == level_now,
            jnp.minimum(accept_margin, at_parent(path_margin)),
            path_margin,
        )
    return (target_lse, token_logprob, residual_mass, accept_margin, path_margin)


def solution(mesh):
    return jax.shard_map(
        body,
        mesh=mesh,
        in_specs=(
            P(("batch", "vocab"), None),
            P(),
            P(None, "vocab"),
            P("batch", "vocab"),
            P("batch"),
            P("batch"),
            P("batch"),
            P("batch"),
        ),
        out_specs=(P("batch"), P("batch"), P("batch"), P("batch"), P("batch")),
        check_vma=False,
    )
```

profile of v0, /device:TPU:0, one launch (start us, length us, event | category | flops | bytes accessed | tf_op | source)
XLA Modules:
  0.0 205.6 jit_solution(12581026114057105658)
XLA Ops:
  7.2 0.7 convert_element_type.16
  7.9 1.1 fusion.41
  9.0 1.8 fusion.43
  10.8 1.9 reduce_max.28
  12.8 0.8 eq.79
  13.5 2.5 %fusion.1 = f32[1024]{0:T(1024)S(1)} fusion(bf16[1024,1024]{1,0:T(8,128)(2,1)} %param.11, f32[1024]{0:T(1024)S(1)} %reduce_max.32), kind=kLoop, calls=%fused_computation.3 | loop fusion | flops 3144704 | bytes 2105344 | tf_op jit(solution)/shard_map/reduce_sum | solution.py:116
  16.0 94.9 %all-gather.2.cloned.1.call-done = bf16[1024,7168]{1,0:T(8,128)(2,1)} async-done(((bf16[16,7168]{1,0:T(8,128)(2,1)}), bf16[1024,7168]{1,0:T(8,128)(2,1)}) %all-gather.2.cloned.1.call-update) | async-done | bytes 14680080 | tf_op jit(solution)/shard_map/all_gather | solution.py:105
  110.9 19.6 %fusion.66 = (f32[1024]{0:T(1024)S(1)}, f32[1024,1024]{1,0:T(8,128)S(1)}) fusion(bf16[1024,7168]{1,0:T(8,128)(2,1)} %all-gather.2.cloned.1.call-done, bf16[7168,1024]{1,0:T(8,128)(2,1)} %param.10), kind=kOutput, calls=%fused_computation.97 | convolution fusion | flops 15033433088 | bytes 33558528 | tf_op jit(solution)/shard_map/dot_general | solution.py:104
  130.5 1.9 copy-done
  132.4 1.1 exponential_reduce_fusion
  133.5 1.2 broadcast_in_dim.6
  134.7 8.8 %all-to-all-start = ((f32[64,4,1024]{2,1,0:T(4,128)}), f32[64,4,1024]{2,1,0:T(4,128)S(1)}, u32[]{:S(2)}, u32[]{:S(2)}) async-start(f32[64,4,1024]{2,1,0:T(4,128)} %broadcast_in_dim.6), calls=%async_computation | async-start | bytes 2097152 | tf_op jit(solution)/shard_map/all_to_all | solution.py:16
  143.5 1.0 fusion.40
  144.5 2.1 copy.24
  146.8 1.4 fusion.27
  148.3 5.1 %fusion.24 = f32[16,64]{1,0:T(8,128)S(1)} fusion(f32[16,64,64]{1,2,0:T(8,128)} %copy.24, f32[16,64,1024]{2,1,0:T(8,128)} %bitcast.73, s32[16,64]{1,0:T(8,128)S(1)} %eq.83, pred[16,64]{1,0:T(8,128)(4,1)S(1)} %and.16), kind=kOutput, calls=%fused_computation.20 | convolution fusion | flops 807533568 | bytes 4465664 | tf_op jit(solution)/shard_map/rnv,rkv->rnk/dot_general | solution.py:124
  153.4 8.5 %all-to-all-done = f32[64,4,1024]{2,1,0:T(4,128)S(1)} async-done(((f32[64,4,1024]{2,1,0:T(4,128)}), f32[64,4,1024]{2,1,0:T(4,128)S(1)}, u32[]{:S(2)}, u32[]{:S(2)}) %all-to-all-start) | async-done | bytes 1048608 | tf_op jit(solution)/shard_map/all_to_all | solution.py:16
  161.9 1.6 fusion.65
  163.6 1.0 copy.65
  166.8 0.7 fusion.63
  167.5 3.6 %fusion.5 = f32[1024]{0:T(1024)S(1)} fusion(bf16[1024,1024]{1,0:T(8,128)(2,1)S(1)} %copy-done.1, f32[1024,1024]{1,0:T(8,128)} %copy-done, f32[1024]{0:T(1024)S(1)} %bitcast.87, f32[1024]{0:T(1024)S(1)} %bitcast.85), kind=kLoop, calls=%fused_computation.7 | loop fusion | flops 6290432 | bytes 6303744 | tf_op jit(solution)/shard_map/reduce_sum | solution.py:140
  171.2 1.3 broadcast_in_dim.7
  172.4 4.9 %all-to-all-start.1 = ((f32[64,1,3072]{2,1,0:T(1,128)}), f32[64,1,3072]{2,1,0:T(1,128)S(1)}, u32[]{:S(2)}, u32[]{:S(2)}) async-start(f32[64,1,3072]{2,1,0:T(1,128)} %broadcast_in_dim.7), calls=%async_computation.1 | async-start | bytes 1572864 | tf_op jit(solution)/shard_map/all_to_all | solution.py:16
  178.1 0.6 fusion.39
  178.8 0.6 fusion.38
  179.5 12.4 %all-to-all-done.1 = f32[64,1,3072]{2,1,0:T(1,128)S(1)} async-done(((f32[64,1,3072]{2,1,0:T(1,128)}), f32[64,1,3072]{2,1,0:T(1,128)S(1)}, u32[]{:S(2)}, u32[]{:S(2)}) %all-to-all-start.1) | async-done | bytes 786464 | tf_op jit(solution)/shard_map/all_to_all | solution.py:16
  192.3 0.6 minimum_select_fusion.7
  193.7 0.6 fusion.35
  195.2 0.6 fusion.33
  196.0 0.6 fusion.32
  196.7 0.6 fusion.31
  198.1 0.6 minimum_select_fusion
  (111 shorter events, 6.7 us)
Async XLA Ops:
  7.2 103.7 %all-gather.2.cloned.1.call-start = ((), (), s32[]{:S(2)}) async-start(), calls=%async_computation.2 | async-start | bytes 14909440 | tf_op jit(solution)/shard_map/all_gather | solution.py:105
  130.5 1.9 copy-start
  132.4 14.2 %copy-start.7 = (s32[1024]{0:T(1024)S(1)}, s32[1024]{0:T(1024)}, u32[]{:S(2)}) copy-start(s32[1024]{0:T(1024)} %param.12) | copy-start | bytes 12292
  132.4 14.3 %copy-start.1 = (bf16[1024,1024]{1,0:T(8,128)(2,1)S(1)}, bf16[1024,1024]{1,0:T(8,128)(2,1)}, u32[]{:S(2)}) copy-start(bf16[1024,1024]{1,0:T(8,128)(2,1)} %param.11) | copy-start | bytes 6291460
  134.7 27.2 %all-to-all-start = ((f32[64,4,1024]{2,1,0:T(4,128)}), f32[64,4,1024]{2,1,0:T(4,128)S(1)}, u32[]{:S(2)}, u32[]{:S(2)}) async-start(f32[64,4,1024]{2,1,0:T(4,128)} %broadcast_in_dim.6), calls=%async_computation | async-start | bytes 2097152 | tf_op jit(solution)/shard_map/all_to_all | solution.py:16
  163.5 1.8 copy-start.2
  167.5 5.0 %copy-start.5 = (f32[1,1024]{1,0:T(1,128)}, f32[1,1024]{1,0:T(1,128)S(1)}, u32[]{:S(2)}) copy-start(f32[1,1024]{1,0:T(1,128)S(1)} %get-tuple-element.42) | copy-start | bytes 12292
  167.5 24.8 %copy-start.3 = (s32[1024]{0:T(1024)S(1)}, s32[1024]{0:T(1024)}, u32[]{:S(2)}) copy-start(s32[1024]{0:T(1024)} %param.14) | copy-start | bytes 12292
  167.5 24.8 %copy-start.6 = (f32[1024]{0:T(1024)S(1)}, f32[1024]{0:T(1024)}, u32[]{:S(2)}) copy-start(f32[1024]{0:T(1024)} %param.15) | copy-start | bytes 12292
  172.4 19.4 %all-to-all-start.1 = ((f32[64,1,3072]{2,1,0:T(1,128)}), f32[64,1,3072]{2,1,0:T(1,128)S(1)}, u32[]{:S(2)}, u32[]{:S(2)}) async-start(f32[64,1,3072]{2,1,0:T(1,128)} %broadcast_in_dim.7), calls=%async_computation.1 | async-start | bytes 1572864 | tf_op jit(solution)/shard_map/all_to_all | solution.py:16
  192.9 5.8 %copy-start.4 = (f32[1024]{0:T(1024)}, f32[1024]{0:T(1024)S(1)}, u32[]{:S(2)}) copy-start(f32[1024]{0:T(1024)S(1)} %get-tuple-element.6) | copy-start | bytes 12292
Sparse Core Ops, SparseCore 0:
  10.9 99.9 all-gather.1
where the time goes:
time: 206 us
  waiting for transfers between devices  116 us (56%)
  matrix products  32 us (16%)
  other arithmetic  16.5 us (8%)
  between operations  14.4 us (7%)
  starting transfers between devices  13.7 us (7%)
  local copies, waits for them, and re-layouts  13.3 us (6%)
    all_gather x1, waiting for transfers between devices, body(): lax.all_gather(normed, 'vocab', axis=0, tiled=True)  94.9 us
    all_to_all x2, waiting for transfers between devices, sent_to_all(): return lax.all_to_all(copies, axis, split_axis=0, concat_axis=0, tiled=True)  20.8 us
    dot_general x1, matrix products, body(): jnp.dot(lax.all_gather(normed, 'vocab', axis=0, tiled=True), lm_head, pre...  19.6 us
    all_to_all x2, starting transfers between devices, sent_to_all(): return lax.all_to_all(copies, axis, split_axis=0, concat_axis=0, tiled=True)  13.7 us
    dot_general x10, matrix products, at_parent(): jnp.einsum('rkn,rn->rk', parent_hot, vector.reshape(requests, NODES), pre...  5.89 us
    unnamed x21, local copies, waits for them, and re-layouts  5.15 us
    dot_general x1, matrix products, body(): jnp.einsum('rnv,rkv->rnk', logits.reshape(requests, NODES, vocab_dev), co...  5.12 us
  transfers between devices with their start and end apart: 3, of which 3 were waited for; matrix products, arithmetic and copies ran while one was open for 8% of the time, Pallas kernels for 0%

commit v1 on v0

v1 whole, which is shorter than its diff:
```python
import heapq
import itertools

import jax
import jax.numpy as jnp
from jax import lax
from jax.experimental import pallas as pl
from jax.experimental.pallas import tpu as pltpu
from jax.sharding import PartitionSpec as P

NODES = 64
DEPTH_MAX = 8
EPSILON = 1e-06
LANES = 128
SIDE = 4
MESH = pl.DeviceIdType.MESH

ROUTES = ((0, 1, 2), (1, 2, 0), (2, 0, 1))
GROUPS = ((2, 4, 4, 4, 4, 1), (2, 4, 4, 4, 4, 1), (2, 4, 4, 4, 3, 1))


def relay_sides():
    sides = {}
    for p, sizes in enumerate(GROUPS):
        for phase in range(3):
            lean = 0
            for g in sorted(range(len(sizes)), key=lambda g: -sizes[g]):
                sides[p, g, phase] = 0 if lean <= 0 else 1
                lean += sizes[g] if lean <= 0 else -sizes[g]
    return sides


SIDES = relay_sides()


def plan():
    rate, latency = 46600.0, 2.2
    free = {(a, d): 0.0 for a in range(3) for d in range(2)}
    coming, count, have, order, ready = [], itertools.count(), set(), [], []

    def send(now, p, g, phase, kind):
        way = (ROUTES[p][phase], kind if kind < 2 else SIDES[p, g, phase])
        free[way] = max(now, free[way]) + GROUPS[p][g] * 4096 * SIDE**phase / rate
        heapq.heappush(coming, (free[way] + latency, next(count), (p, g, phase, kind)))

    now = 0.0
    for g in range(max(map(len, GROUPS))):
        for p in range(3):
            if g < len(GROUPS[p]):
                send(now, p, g, 0, 0)
                send(now, p, g, 0, 1)
    while coming or ready:
        if coming and (coming[0][0] <= now or not ready):
            at, _, message = heapq.heappop(coming)
            now = max(now, at) + 0.03
            p, g, phase, kind = message
            have.add(message)
            order.append(("take", message))
            if kind == SIDES[p, g, phase]:
                send(now, p, g, phase, 2)
            if all((p, g, phase, k) in have for k in range(3)):
                if phase < 2:
                    send(now, p, g, phase + 1, 0)
                    send(now, p, g, phase + 1, 1)
                else:
                    ready.append((p, g))
        else:
            p, g = ready.pop(0)
            order.append(("multiply", (p, g)))
            now += 0.27 * max(2, GROUPS[p][g])
    return order


ORDER = plan()
PAIRS = [(p, g) for kind, (p, g, *_) in ORDER if kind == "multiply"]
MESSAGES = [m for kind, m in ORDER if kind == "take"]
FIRST_TILE = {
    (p, g): sum(map(sum, GROUPS[:p])) + sum(GROUPS[p][:g]) for p in range(3) for g in range(len(GROUPS[p]))
}


def as_column(row):
    return jnp.transpose(jnp.broadcast_to(row, (LANES, LANES)))


def main_kernel(
    hidden_hbm, gain_hbm, head_hbm, draft_hbm, tokens_hbm, parents_hbm,
    out_ref,
    hidden_ref, gain_ref, head_ref, draft_ref, tokens_ref, parents_ref,
    rows_ref, logits_ref, weight_ref, draft_prob_ref, stat_ref, pair_ref, triple_ref,
    small_sem, head_sem, send_sem, take_sem, swap_send_sem, swap_take_sem,
):
    me = lax.axis_index("vocab")
    batch = lax.axis_index("batch")
    at = (me // 16, (me // 4) % 4, me % 4)
    stride = (16, 4, 1)
    width = logits_ref.shape[1]
    spans = logits_ref.shape[0] // LANES

    def peer(axis, step):
        return (me + (lax.rem(at[axis] + step, SIDE) - at[axis]) * stride[axis], batch)

    small = [
        pltpu.make_async_copy(src, dst, small_sem.at[k])
        for k, (src, dst) in enumerate(
            (
                (hidden_hbm, hidden_ref),
                (gain_hbm, gain_ref),
                (draft_hbm, draft_ref),
                (tokens_hbm, tokens_ref),
                (parents_hbm, parents_ref),
            )
        )
    ]
    for copy in small:
        copy.start()
    barrier = pltpu.get_barrier_semaphore()
    for axis in range(3):
        for step in (1, 2, 3):
            pl.semaphore_signal(barrier, inc=1, device_id=peer(axis, step), device_id_type=MESH)
    head_copies = {}
    for k, pair in enumerate(PAIRS):
        span = pl.ds(FIRST_TILE[pair] * LANES, GROUPS[pair[0]][pair[1]] * LANES)
        head_copies[pair] = pltpu.make_async_copy(head_hbm.at[span], head_ref.at[span], head_sem.at[k])
        head_copies[pair].start()

    small[0].wait()
    small[1].wait()
    tiles = hidden_ref.shape[1] // LANES
    squares = jnp.zeros((16, LANES), jnp.float32)
    for k in range(tiles):
        part = hidden_ref[:, k * LANES : (k + 1) * LANES].astype(jnp.float32)
        squares += part * part
    scale = lax.rsqrt(jnp.sum(squares, axis=1, keepdims=True) / hidden_ref.shape[1] + EPSILON)
    for k in range(tiles):
        part = hidden_ref[:, k * LANES : (k + 1) * LANES].astype(jnp.float32)
        gain = gain_ref[:, k * LANES : (k + 1) * LANES].astype(jnp.float32)
        rows_ref[k, at[0], at[1], at[2]] = (part * scale * gain).astype(jnp.bfloat16)
    pl.semaphore_wait(barrier, 9)

    number = {m: k for k, m in enumerate(MESSAGES)}
    sent = []

    def message(p, g, phase, kind, taking):
        axis = ROUTES[p][phase]
        side = kind if kind < 2 else SIDES[p, g, phase]
        up = 1 if side == 0 else 3
        begun = (SIDE - up) * (2 if kind == 2 else 1) if taking else ((SIDE - up) if kind == 2 else 0)
        index = [pl.ds(FIRST_TILE[p, g], GROUPS[p][g]), *at]
        for done in range(phase):
            index[1 + ROUTES[p][done]] = pl.ds(0, SIDE)
        index[1 + axis] = lax.rem(at[axis] + begun, SIDE)
        block = rows_ref.at[tuple(index)]
        k = number[p, g, phase, kind]
        return pltpu.make_async_remote_copy(
            src_ref=block,
            dst_ref=block,
            send_sem=send_sem.at[k],
            recv_sem=take_sem.at[k],
            device_id=peer(axis, up),
            device_id_type=MESH,
        )

    def send(*key):
        copy = message(*key, False)
        copy.start()
        sent.append(copy)

    def multiply(p, g):
        first, many = FIRST_TILE[p, g], GROUPS[p][g]
        head_copies[p, g].wait()

        def strip(n, carry):
            columns = pl.ds(pl.multiple_of(n * 256, 256), 256)
            left = jnp.concatenate(
                [rows_ref[first + k].reshape(logits_ref.shape[0], LANES) for k in range(many)], axis=1
            )
            logits_ref[:, columns] += jnp.dot(
                left, head_ref[first * LANES : (first + many) * LANES, columns], preferred_element_type=jnp.float32
            )
            return carry

        lax.fori_loop(0, width // 256, strip, 0)

    def put(ref, stage, axis, values):
        for k, value in enumerate(values):
            ref[stage, at[axis], k] = value

    def swap(ref, stage, number_of, axis):
        copies = []
        for step in (1, 2, 3):
            block = ref.at[stage, at[axis]]
            copy = pltpu.make_async_remote_copy(
                src_ref=block,
                dst_ref=block,
                send_sem=swap_send_sem.at[number_of, step - 1],
                recv_sem=swap_take_sem.at[number_of, step - 1],
                device_id=peer(axis, step),
                device_id_type=MESH,
            )
            copy.start()
            copies.append(copy)
        sent.extend(copies)
        return copies

    def taken(ref, stage, number_of, axis):
        for step in (1, 2, 3):
            block = ref.at[stage, lax.rem(at[axis] + SIDE - step, SIDE)]
            pltpu.make_async_remote_copy(
                src_ref=block,
                dst_ref=block,
                send_sem=swap_send_sem.at[number_of, step - 1],
                recv_sem=swap_take_sem.at[number_of, step - 1],
                device_id=peer(axis, step),
                device_id_type=MESH,
            ).wait_recv()

    def joined_pair(stage):
        tops = [pair_ref[stage, c, 0] for c in range(SIDE)]
        top = jnp.maximum(jnp.maximum(tops[0], tops[1]), jnp.maximum(tops[2], tops[3]))
        total = sum(pair_ref[stage, c, 1] * jnp.exp(tops[c] - top) for c in range(SIDE))
        return top, total

    def summed(stage):
        return [sum(triple_ref[stage, c, k] for c in range(SIDE)) for k in range(3)]

    def rows_of(b):
        return pl.ds(pl.multiple_of(b * LANES, LANES), LANES)

    def stat_row(k, b):
        return stat_ref[k, pl.ds(b, 1), :]

    def set_stat(k, b, value):
        stat_ref[k, pl.ds(b, 1), :] = value

    def down(matrix, combine):
        return combine(jnp.transpose(matrix), axis=0, keepdims=True)

    lane = lax.broadcasted_iota(jnp.int32, (LANES, LANES), 1).astype(jnp.float32)

    def pickers(b):
        parent = as_column(parents_ref[pl.ds(b, 1), :].astype(jnp.float32))
        below = (lax.broadcasted_iota(jnp.int32, (LANES, LANES), 0) // NODES * NODES).astype(jnp.float32)
        hot = jnp.where(parent + below == lane, 1.0, 0.0).astype(jnp.bfloat16)
        token = as_column((tokens_ref[pl.ds(b, 1), :] - me * width).astype(jnp.float32))
        return hot, token

    def picked(pieces, hot, token):
        total = jnp.zeros((LANES, LANES), jnp.float32)
        for c in range(width // 256):
            found = sum(
                jnp.dot(hot, piece, preferred_element_type=jnp.float32)
                for piece in pieces(slice(c * 256, (c + 1) * 256))
            )
            for half in range(2):
                here = found[:, half * LANES : (half + 1) * LANES]
                total += jnp.where(token == lane + float(c * 256 + half * LANES), here, 0.0)
        return total

    def column_tiles():
        return [slice(c * LANES, (c + 1) * LANES) for c in range(width // LANES)]

    def draft_stats(b, carry):
        rows = rows_of(b)
        top = jnp.full((LANES, LANES), -jnp.inf, jnp.float32)
        for tile in column_tiles():
            top = jnp.maximum(top, draft_ref[rows, tile].astype(jnp.float32))
        top = down(top, jnp.max)
        column = as_column(top)
        total = jnp.zeros((LANES, LANES), jnp.float32)
        for tile in column_tiles():
            total += jnp.exp(draft_ref[rows, tile].astype(jnp.float32) - column)
        set_stat(0, b, top)
        set_stat(1, b, down(total, jnp.sum))
        hot, token = pickers(b)
        set_stat(2, b, down(picked(lambda tile: [draft_ref[rows, tile]], hot, token), jnp.sum))
        return carry

    def draft_probs(b, carry):
        rows = rows_of(b)
        column = as_column(stat_row(6, b))
        for tile in column_tiles():
            draft_prob_ref[rows, tile] = jnp.exp(draft_ref[rows, tile].astype(jnp.float32) - column)
        return carry

    def target_stats(b, carry):
        rows = rows_of(b)
        top = jnp.full((LANES, LANES), -jnp.inf, jnp.float32)
        for tile in column_tiles():
            top = jnp.maximum(top, logits_ref[rows, tile])
        top = down(top, jnp.max)
        column = as_column(top)
        total = jnp.zeros((LANES, LANES), jnp.float32)
        for tile in column_tiles():
            weight = jnp.exp(logits_ref[rows, tile] - column)
            weight_ref[rows, tile] = weight
            total += weight
        set_stat(3, b, top)
        set_stat(4, b, down(total, jnp.sum))
        return carry

    def target_picks(b, carry):
        rows = rows_of(b)

        def pieces(tile):
            values = logits_ref[rows, tile]
            high = values.astype(jnp.bfloat16)
            rest = values - high.astype(jnp.float32)
            middle = rest.astype(jnp.bfloat16)
            low = (rest - middle.astype(jnp.float32)).astype(jnp.bfloat16)
            return high, middle, low

        hot, token = pickers(b)
        set_stat(5, b, down(picked(pieces, hot, token), jnp.sum))
        return carry

    def residuals(b, carry):
        rows = rows_of(b)
        factor = as_column(stat_row(7, b))
        total = jnp.zeros((LANES, LANES), jnp.float32)
        for tile in column_tiles():
            total += jnp.maximum(weight_ref[rows, tile] * factor - draft_prob_ref[rows, tile], 0.0)
        set_stat(8, b, down(total, jnp.sum))
        return carry

    def over(body, low=0, high=spans):
        lax.fori_loop(low, high, body, 0)

    def draft_work():
        for c in (2, 3, 4):
            small[c].wait()
        yield
        for b in range(0, spans, 2):
            over(draft_stats, b, b + 2)
            yield
        put(pair_ref, 0, 0, (stat_ref[0], stat_ref[1]))
        yield
        swap(pair_ref, 0, 0, 0)
        yield
        for axis in (1, 2):
            yield
            yield
            taken(pair_ref, axis - 1, axis - 1, axis - 1)
            put(pair_ref, axis, axis, joined_pair(axis - 1))
            yield
            swap(pair_ref, axis, axis, axis)
            yield
        yield
        yield
        taken(pair_ref, 2, 2, 2)
        top, total = joined_pair(2)
        stat_ref[6] = top + jnp.log(total)
        for b in range(0, spans, 4):
            yield
            over(draft_probs, b, b + 4)

    for g in range(max(map(len, GROUPS))):
        for p in range(3):
            if g < len(GROUPS[p]):
                send(p, g, 0, 0)
                send(p, g, 0, 1)
    def clear(b, carry):
        logits_ref[rows_of(b)] = jnp.zeros((LANES, width), jnp.float32)
        return carry

    over(clear)
    have = set()
    draft = draft_work()
    for step, (kind, key) in enumerate(ORDER):
        if kind == "multiply":
            multiply(*key)
            continue
        message(*key, True).wait_recv()
        p, g, phase, way = key
        have.add(key)
        if way == SIDES[p, g, phase]:
            send(p, g, phase, 2)
        if phase < 2 and all((p, g, phase, k) in have for k in range(3)):
            send(p, g, phase + 1, 0)
            send(p, g, phase + 1, 1)
        if step >= 24 and step % 3 == 0:
            next(draft, None)
    for _ in draft:
        pass

    over(target_stats)
    put(pair_ref, 3, 0, (stat_ref[3], stat_ref[4]))
    swap(pair_ref, 3, 3, 0)
    over(target_picks, 0, spans // 2)
    taken(pair_ref, 3, 3, 0)
    put(pair_ref, 4, 1, joined_pair(3))
    swap(pair_ref, 4, 4, 1)
    over(target_picks, spans // 2, spans)
    taken(pair_ref, 4, 4, 1)
    put(pair_ref, 5, 2, joined_pair(4))
    swap(pair_ref, 5, 5, 2)
    taken(pair_ref, 5, 5, 2)
    top, total = joined_pair(5)
    target_lse = top + jnp.log(total)
    stat_ref[7] = jnp.exp(stat_ref[3] - target_lse)
    over(residuals)
    values = (stat_ref[8], stat_ref[5], stat_ref[2])
    for axis in range(3):
        put(triple_ref, axis, axis, values)
        swap(triple_ref, axis, 6 + axis, axis)
        taken(triple_ref, axis, 6 + axis, axis)
        values = summed(axis)
    out_ref[0] = target_lse
    out_ref[1] = stat_ref[6]
    for k in range(3):
        out_ref[2 + k] = values[k]
    for copy in sent:
        copy.wait_send()


def tree_kernel(stats_ref, parents_ref, depths_ref, uniforms_ref, lse_ref, token_ref, residual_ref, accept_ref, path_ref):
    lanes = lax.broadcasted_iota(jnp.int32, parents_ref.shape, 1)
    parent = lanes // NODES * NODES + parents_ref[...]

    def at_parent(vector):
        return jnp.take_along_axis(vector, parent, axis=1)

    target_lse = stats_ref[0]
    token_logprob = stats_ref[3] - at_parent(target_lse)
    draft_logprob = stats_ref[4] - at_parent(stats_ref[1])
    accept = jnp.exp(jnp.minimum(token_logprob - draft_logprob, 0.0)) - uniforms_ref[...]
    depths = depths_ref[...]
    path = jnp.ones(accept.shape, jnp.float32)
    for level in range(1, DEPTH_MAX + 1):
        path = jnp.where(depths == level, jnp.minimum(accept, at_parent(path)), path)
    lse_ref[...] = target_lse
    token_ref[...] = token_logprob
    residual_ref[...] = stats_ref[2]
    accept_ref[...] = accept
    path_ref[...] = path


def body(hidden, norm_gain, lm_head, draft_logits, draft_tokens, tree_parents, node_depths, uniforms):
    depth, width = lm_head.shape
    rows = draft_logits.shape[0]
    spans = rows // LANES
    flat = (spans, LANES)
    hbm = pl.BlockSpec(memory_space=pltpu.HBM)
    vmem = pl.BlockSpec(memory_space=pltpu.VMEM)
    stats = pl.pallas_call(
        main_kernel,
        out_shape=jax.ShapeDtypeStruct((5, *flat), jnp.float32),
        in_specs=[hbm] * 6,
        out_specs=vmem,
        scratch_shapes=[
            pltpu.VMEM(hidden.shape, jnp.bfloat16),
            pltpu.VMEM((1, depth), jnp.bfloat16),
            pltpu.VMEM((depth, width), jnp.bfloat16),
            pltpu.VMEM((rows, width), jnp.bfloat16),
            pltpu.VMEM(flat, jnp.int32),
            pltpu.VMEM(flat, jnp.int32),
            pltpu.VMEM((depth // LANES, SIDE, SIDE, SIDE, hidden.shape[0], LANES), jnp.bfloat16),
            pltpu.VMEM((rows, width), jnp.float32),
            pltpu.VMEM((rows, width), jnp.float32),
            pltpu.VMEM((rows, width), jnp.float32),
            pltpu.VMEM((9, *flat), jnp.float32),
            pltpu.VMEM((6, SIDE, 2, *flat), jnp.float32),
            pltpu.VMEM((3, SIDE, 3, *flat), jnp.float32),
            pltpu.SemaphoreType.DMA((5,)),
            pltpu.SemaphoreType.DMA((len(PAIRS),)),
            pltpu.SemaphoreType.DMA((len(MESSAGES),)),
            pltpu.SemaphoreType.DMA((len(MESSAGES),)),
            pltpu.SemaphoreType.DMA((9, 3)),
            pltpu.SemaphoreType.DMA((9, 3)),
        ],
        compiler_params=pltpu.CompilerParams(
            collective_id=0, has_side_effects=True, vmem_limit_bytes=60 * 2**20
        ),
        name="gather_verify",
    )(
        hidden,
        norm_gain.reshape(1, depth),
        lm_head,
        draft_logits,
        draft_tokens.reshape(flat),
        tree_parents.reshape(flat),
    )
    outs = pl.pallas_call(
        tree_kernel,
        out_shape=[jax.ShapeDtypeStruct(flat, jnp.float32)] * 5,
        in_specs=[vmem] * 4,
        out_specs=[vmem] * 5,
        name="tree",
    )(stats, tree_parents.reshape(flat), node_depths.reshape(flat), uniforms.reshape(flat))
    return tuple(out.reshape(rows) for out in outs)


def solution(mesh):
    return jax.shard_map(
        body,
        mesh=mesh,
        in_specs=(
            P(("batch", "vocab"), None),
            P(),
            P(None, "vocab"),
            P("batch", "vocab"),
            P("batch"),
            P("batch"),
            P("batch"),
            P("batch"),
        ),
        out_specs=(P("batch"), P("batch"), P("batch"), P("batch"), P("batch")),
        check_vma=False,
    )
```

time: 206 us -> 124 us (0.60)
  Pallas kernels: 0 us -> 122 us
  waiting for transfers between devices: 116 us -> 0 us
  matrix products: 32 us -> 0 us
  other arithmetic: 16.5 us -> 0 us
  between operations: 14.4 us -> 0.64 us
  starting transfers between devices: 13.7 us -> 0 us
  local copies, waits for them, and re-layouts: 13.3 us -> 1.35 us
    pallas_call x0 -> x2, Pallas kernels: none -> 122 us  [the longest x1 120 us: body(): pl.pallas_call(main_kernel, out_shape=jax.ShapeDtypeStruct((5, *flat), jn...]
    all_gather x1 -> x0, waiting for transfers between devices: 94.9 us -> none  [body(): lax.all_gather(normed, 'vocab', axis=0, tiled=True)]
    dot_general x13 -> x0, matrix products: 32 us -> none  [the longest x1 19.6 us: body(): jnp.dot(lax.all_gather(normed, 'vocab', axis=0, tiled=True), lm_head, pre...]
    all_to_all x2 -> x0, waiting for transfers between devices: 20.8 us -> none  [sent_to_all(): return lax.all_to_all(copies, axis, split_axis=0, concat_axis=0, tiled=True)]
    all_to_all x2 -> x0, starting transfers between devices: 13.7 us -> none  [sent_to_all(): return lax.all_to_all(copies, axis, split_axis=0, concat_axis=0, tiled=True)]
    reduce_sum x5 -> x0, other arithmetic: 8.74 us -> none  [the longest x1 3.63 us: body(): jnp.sum(excess, axis=1)]
    unnamed x21 -> x0, local copies, waits for them, and re-layouts: 5.15 us -> none
    slice x41 -> x0, local copies, waits for them, and re-layouts: 2.66 us -> none  [the longest x1 1.55 us: collected_together(): share = both[:, at:at + len(line)].reshape(len(both), -1)]
  transfers between devices with their start and end apart: 3 -> 0, of which waited for: 3 -> 0; matrix products, arithmetic and copies ran while one was open for 8% -> 0% of each run, Pallas kernels for 0% -> 0%
where the time goes in v1:
time: 124 us
  Pallas kernels  122 us (98%)
  local copies, waits for them, and re-layouts  1.35 us (1%)
    pallas_call x1, Pallas kernels, body(): pl.pallas_call(main_kernel, out_shape=jax.ShapeDtypeStruct((5, *flat), jn...  120 us

profile of v1, /device:TPU:0, one launch (start us, length us, event | category | flops | bytes accessed | tf_op | source)
XLA Modules:
  0.0 123.8 jit_solution(10843988461383777798)
XLA Ops:
  0.6 1.3 %reshape.41.gain_hbm = bf16[1,7168]{1,0:T(2,128)(2,1)} reshape(bf16[7168]{0:T(1024)(128)(2,1)} %param.9) | data formatting | bytes 28672 | tf_op jit(solution)/shard_map/reshape | solution.py:477
  2.0 119.9 %gather_verify.1.stats_ref = f32[5,8,128]{2,1,0:T(8,128)} custom-call(bf16[16,7168]{1,0:T(8,128)(2,1)} %hidden_hbm.1, bf16[1,7168]{1,0:T(2,128)(2,1)} %reshape.41.gain_hbm, bf16[7168,1024]{1,0:T(8,128)(2,1)} %head_hbm.1, bf16[1024,1024]{1,0:T(8,128)(2,1)} %draft_hbm.1, s32[8,128]{1,0:T(8,128)} %bitcast.11, s32[8,128]{1,0:T(8,128)} %bitcast.9), custom_call_target="tpu_custom_call" | custom-call | tf_op jit(solution)/shard_map/gather_verify/pallas_call | solution.py:445
  121.9 1.9 %tree.1 = (f32[8,128]{1,0:T(8,128)}, f32[8,128]{1,0:T(8,128)}, f32[8,128]{1,0:T(8,128)}, f32[8,128]{1,0:T(8,128)}, f32[8,128]{1,0:T(8,128)}) custom-call(f32[5,8,128]{2,1,0:T(8,128)} %gather_verify.1.stats_ref, s32[8,128]{1,0:T(8,128)} %bitcast.10, s32[8,128]{1,0:T(8,128)} %bitcast.12, f32[8,128]{1,0:T(8,128)} %bitcast.13), custom_call_target="tpu_custom_call" | custom-call | tf_op jit(solution)/shard_map/tree/pallas_call | solution.py:483

commit v2 on v1

--- a/solution.py
+++ b/solution.py
@@ -33,26 +33,36 @@
 SIDES = relay_sides()
 
 
+DRAFT = (
+    [(("stats", b), 0.45, 2.0 if b == 0 else 0.0) for b in range(8)]
+    + [(("join", axis), 0.3, 12.0 if axis else 0.0) for axis in range(4)]
+    + [(("probs", b), 0.2, 0.0) for b in range(8)]
+)
+STRIPS = 2
+
+
 def plan():
-    rate, latency = 46600.0, 2.2
+    rate, gap, latency = 44500.0, 0.2, 2.5
     free = {(a, d): 0.0 for a in range(3) for d in range(2)}
     coming, count, have, order, ready = [], itertools.count(), set(), [], []
+    draft = list(DRAFT)
 
     def send(now, p, g, phase, kind):
         way = (ROUTES[p][phase], kind if kind < 2 else SIDES[p, g, phase])
-        free[way] = max(now, free[way]) + GROUPS[p][g] * 4096 * SIDE**phase / rate
+        free[way] = max(now, free[way]) + gap + GROUPS[p][g] * 4096 * SIDE**phase / rate
         heapq.heappush(coming, (free[way] + latency, next(count), (p, g, phase, kind)))
 
-    now = 0.0
+    now, last = 0.0, 0.0
     for g in range(max(map(len, GROUPS))):
         for p in range(3):
             if g < len(GROUPS[p]):
                 send(now, p, g, 0, 0)
                 send(now, p, g, 0, 1)
-    while coming or ready:
-        if coming and (coming[0][0] <= now or not ready):
+    while coming or ready or draft:
+        due = last + draft[0][2] if draft else float("inf")
+        if coming and coming[0][0] <= now or not ready and coming and coming[0][0] <= due:
             at, _, message = heapq.heappop(coming)
-            now = max(now, at) + 0.03
+            now = max(now, at) + 0.05
             p, g, phase, kind = message
             have.add(message)
             order.append(("take", message))
@@ -63,16 +73,20 @@
                     send(now, p, g, phase + 1, 0)
                     send(now, p, g, phase + 1, 1)
                 else:
-                    ready.append((p, g))
+                    ready.extend((p, g, n) for n in range(STRIPS))
+        elif draft and (due <= now or not ready):
+            what, cost, _ = draft.pop(0)
+            order.append(("draft", what))
+            now = last = max(now, due) + cost
         else:
-            p, g = ready.pop(0)
-            order.append(("multiply", (p, g)))
-            now += 0.27 * max(2, GROUPS[p][g])
+            p, g, n = ready.pop(0)
+            order.append(("multiply", (p, g, n)))
+            now += 0.05 + 0.32 / STRIPS * max(2, GROUPS[p][g])
     return order
 
 
 ORDER = plan()
-PAIRS = [(p, g) for kind, (p, g, *_) in ORDER if kind == "multiply"]
+PAIRS = [key[:2] for kind, key in ORDER if kind == "multiply" and key[2] == 0]
 MESSAGES = [m for kind, m in ORDER if kind == "take"]
 FIRST_TILE = {
     (p, g): sum(map(sum, GROUPS[:p])) + sum(GROUPS[p][:g]) for p in range(3) for g in range(len(GROUPS[p]))
@@ -87,8 +101,8 @@
     hidden_hbm, gain_hbm, head_hbm, draft_hbm, tokens_hbm, parents_hbm,
     out_ref,
     hidden_ref, gain_ref, head_ref, draft_ref, tokens_ref, parents_ref,
-    rows_ref, logits_ref, weight_ref, draft_prob_ref, stat_ref, pair_ref, triple_ref,
-    small_sem, head_sem, send_sem, take_sem, swap_send_sem, swap_take_sem,
+    rows_ref, logits_ref, weight_ref, draft_prob_ref, stat_ref, pair_ref, bank_ref,
+    small_sem, head_sem, send_sem, take_sem, swap_send_sem, swap_take_sem, far_send_sem, far_take_sem,
 ):
     me = lax.axis_index("vocab")
     batch = lax.axis_index("batch")
@@ -134,7 +148,7 @@
     scale = lax.rsqrt(jnp.sum(squares, axis=1, keepdims=True) / hidden_ref.shape[1] + EPSILON)
     for k in range(tiles):
         part = hidden_ref[:, k * LANES : (k + 1) * LANES].astype(jnp.float32)
-        gain = gain_ref[:, k * LANES : (k + 1) * LANES].astype(jnp.float32)
+        gain = gain_ref[k : k + 1, :].astype(jnp.float32)
         rows_ref[k, at[0], at[1], at[2]] = (part * scale * gain).astype(jnp.bfloat16)
     pl.semaphore_wait(barrier, 9)
 
@@ -166,21 +180,21 @@
         copy.start()
         sent.append(copy)
 
-    def multiply(p, g):
+    def multiply(p, g, n):
         first, many = FIRST_TILE[p, g], GROUPS[p][g]
-        head_copies[p, g].wait()
-
-        def strip(n, carry):
-            columns = pl.ds(pl.multiple_of(n * 256, 256), 256)
-            left = jnp.concatenate(
-                [rows_ref[first + k].reshape(logits_ref.shape[0], LANES) for k in range(many)], axis=1
-            )
-            logits_ref[:, columns] += jnp.dot(
-                left, head_ref[first * LANES : (first + many) * LANES, columns], preferred_element_type=jnp.float32
-            )
-            return carry
-
-        lax.fori_loop(0, width // 256, strip, 0)
+        if n == 0:
+            head_copies[p, g].wait()
+        columns = slice(n * width // STRIPS, (n + 1) * width // STRIPS)
+        left = jnp.concatenate(
+            [rows_ref[first + k].reshape(logits_ref.shape[0], LANES) for k in range(many)], axis=1
+        )
+        product = jnp.dot(
+            left, head_ref[first * LANES : (first + many) * LANES, columns], preferred_element_type=jnp.float32
+        )
+        if (p, g) == PAIRS[0]:
+            logits_ref[:, columns] = product
+        else:
+            logits_ref[:, columns] += product
 
     def put(ref, stage, axis, values):
         for k, value in enumerate(values):
@@ -219,10 +233,45 @@
         tops = [pair_ref[stage, c, 0] for c in range(SIDE)]
         top = jnp.maximum(jnp.maximum(tops[0], tops[1]), jnp.maximum(tops[2], tops[3]))
         total = sum(pair_ref[stage, c, 1] * jnp.exp(tops[c] - top) for c in range(SIDE))
-        return top, total
-
-    def summed(stage):
-        return [sum(triple_ref[stage, c, k] for c in range(SIDE)) for k in range(3)]
+        return top, total, sum(pair_ref[stage, c, 2] for c in range(SIDE))
+
+    shifts = sorted(
+        (o for o in itertools.product(range(SIDE), repeat=3) if any(o)), key=lambda o: -sum(min(v, SIDE - v) for v in o)
+    )
+
+    def across(turn, k, back):
+        there = me
+        for axis in range(3):
+            step = shifts[k][axis]
+            here = lax.rem(at[axis] + (SIDE - step if back else step), SIDE)
+            there = there + (here - at[axis]) * stride[axis]
+        block = bank_ref.at[turn, there if back else me]
+        return pltpu.make_async_remote_copy(
+            src_ref=block,
+            dst_ref=block,
+            send_sem=far_send_sem.at[turn, k],
+            recv_sem=far_take_sem.at[turn, k],
+            device_id=(there, batch),
+            device_id_type=MESH,
+        )
+
+    def cast(turn, value):
+        bank_ref[turn, me] = value
+        for k in range(len(shifts)):
+            copy = across(turn, k, False)
+            copy.start()
+            sent.append(copy)
+
+    def collected(turn):
+        for k in range(len(shifts)):
+            across(turn, k, True).wait_recv()
+        return [bank_ref[turn, v] for v in range(len(shifts) + 1)]
+
+    def joined_lse(values):
+        top = values[0]
+        for value in values[1:]:
+            top = jnp.maximum(top, value)
+        return top + jnp.log(sum(jnp.exp(value - top) for value in values))
 
     def rows_of(b):
         return pl.ds(pl.multiple_of(b * LANES, LANES), LANES)
@@ -323,92 +372,61 @@
         set_stat(8, b, down(total, jnp.sum))
         return carry
 
-    def over(body, low=0, high=spans):
-        lax.fori_loop(low, high, body, 0)
-
-    def draft_work():
-        for c in (2, 3, 4):
-            small[c].wait()
-        yield
-        for b in range(0, spans, 2):
-            over(draft_stats, b, b + 2)
-            yield
-        put(pair_ref, 0, 0, (stat_ref[0], stat_ref[1]))
-        yield
-        swap(pair_ref, 0, 0, 0)
-        yield
-        for axis in (1, 2):
-            yield
-            yield
-            taken(pair_ref, axis - 1, axis - 1, axis - 1)
-            put(pair_ref, axis, axis, joined_pair(axis - 1))
-            yield
-            swap(pair_ref, axis, axis, axis)
-            yield
-        yield
-        yield
-        taken(pair_ref, 2, 2, 2)
-        top, total = joined_pair(2)
-        stat_ref[6] = top + jnp.log(total)
-        for b in range(0, spans, 4):
-            yield
-            over(draft_probs, b, b + 4)
+    def over(body, unroll):
+        lax.fori_loop(0, spans, body, 0, unroll=unroll)
+
+    def work_on_draft(what, which):
+        if what == "stats":
+            if which == 0:
+                for copy in small[2:]:
+                    copy.wait()
+            draft_stats(which, 0)
+        elif what == "probs":
+            draft_probs(which, 0)
+        else:
+            if which:
+                taken(pair_ref, which - 1, which - 1, which - 1)
+            values = joined_pair(which - 1) if which else (stat_ref[0], stat_ref[1], stat_ref[2])
+            if which < 3:
+                put(pair_ref, which, which, values)
+                swap(pair_ref, which, which, which)
+            else:
+                stat_ref[6] = values[0] + jnp.log(values[1])
+                out_ref[1] = stat_ref[6]
+                out_ref[4] = values[2]
 
     for g in range(max(map(len, GROUPS))):
         for p in range(3):
             if g < len(GROUPS[p]):
                 send(p, g, 0, 0)
                 send(p, g, 0, 1)
-    def clear(b, carry):
-        logits_ref[rows_of(b)] = jnp.zeros((LANES, width), jnp.float32)
-        return carry
-
-    over(clear)
     have = set()
-    draft = draft_work()
-    for step, (kind, key) in enumerate(ORDER):
+    for kind, key in ORDER:
         if kind == "multiply":
             multiply(*key)
-            continue
-        message(*key, True).wait_recv()
-        p, g, phase, way = key
-        have.add(key)
-        if way == SIDES[p, g, phase]:
-            send(p, g, phase, 2)
-        if phase < 2 and all((p, g, phase, k) in have for k in range(3)):
-            send(p, g, phase + 1, 0)
-            send(p, g, phase + 1, 1)
-        if step >= 24 and step % 3 == 0:
-            next(draft, None)
-    for _ in draft:
-        pass
-
-    over(target_stats)
-    put(pair_ref, 3, 0, (stat_ref[3], stat_ref[4]))
-    swap(pair_ref, 3, 3, 0)
-    over(target_picks, 0, spans // 2)
-    taken(pair_ref, 3, 3, 0)
-    put(pair_ref, 4, 1, joined_pair(3))
-    swap(pair_ref, 4, 4, 1)
-    over(target_picks, spans // 2, spans)
-    taken(pair_ref, 4, 4, 1)
-    put(pair_ref, 5, 2, joined_pair(4))
-    swap(pair_ref, 5, 5, 2)
-    taken(pair_ref, 5, 5, 2)
-    top, total = joined_pair(5)
-    target_lse = top + jnp.log(total)
+        elif kind == "draft":
+            work_on_draft(*key)
+        else:
+            message(*key, True).wait_recv()
+            p, g, phase, way = key
+            have.add(key)
+            if way == SIDES[p, g, phase]:
+                send(p, g, phase, 2)
+            if phase < 2 and all((p, g, phase, k) in have for k in range(3)):
+                send(p, g, phase + 1, 0)
+                send(p, g, phase + 1, 1)
+
+    over(target_stats, spans)
+    cast(0, stat_ref[3] + jnp.log(stat_ref[4]))
+    over(target_picks, 2)
+    cast(1, stat_ref[5])
+    target_lse = joined_lse(collected(0))
     stat_ref[7] = jnp.exp(stat_ref[3] - target_lse)
-    over(residuals)
-    values = (stat_ref[8], stat_ref[5], stat_ref[2])
-    for axis in range(3):
-        put(triple_ref, axis, axis, values)
-        swap(triple_ref, axis, 6 + axis, axis)
-        taken(triple_ref, axis, 6 + axis, axis)
-        values = summed(axis)
+    over(residuals, spans)
+    cast(2, stat_ref[8])
     out_ref[0] = target_lse
-    out_ref[1] = stat_ref[6]
-    for k in range(3):
-        out_ref[2 + k] = values[k]
+    out_ref[3] = sum(collected(1))
+    out_ref[2] = sum(collected(2))
     for copy in sent:
         copy.wait_send()
 
@@ -449,7 +467,7 @@
         out_specs=vmem,
         scratch_shapes=[
             pltpu.VMEM(hidden.shape, jnp.bfloat16),
-            pltpu.VMEM((1, depth), jnp.bfloat16),
+            pltpu.VMEM((depth // LANES, LANES), jnp.bfloat16),
             pltpu.VMEM((depth, width), jnp.bfloat16),
             pltpu.VMEM((rows, width), jnp.bfloat16),
             pltpu.VMEM(flat, jnp.int32),
@@ -459,14 +477,16 @@
             pltpu.VMEM((rows, width), jnp.float32),
             pltpu.VMEM((rows, width), jnp.float32),
             pltpu.VMEM((9, *flat), jnp.float32),
-            pltpu.VMEM((6, SIDE, 2, *flat), jnp.float32),
             pltpu.VMEM((3, SIDE, 3, *flat), jnp.float32),
+            pltpu.VMEM((3, SIDE**3, *flat), jnp.float32),
             pltpu.SemaphoreType.DMA((5,)),
             pltpu.SemaphoreType.DMA((len(PAIRS),)),
             pltpu.SemaphoreType.DMA((len(MESSAGES),)),
             pltpu.SemaphoreType.DMA((len(MESSAGES),)),
-            pltpu.SemaphoreType.DMA((9, 3)),
-            pltpu.SemaphoreType.DMA((9, 3)),
+            pltpu.SemaphoreType.DMA((3, 3)),
+            pltpu.SemaphoreType.DMA((3, 3)),
+            pltpu.SemaphoreType.DMA((3, SIDE**3 - 1)),
+            pltpu.SemaphoreType.DMA((3, SIDE**3 - 1)),
         ],
         compiler_params=pltpu.CompilerParams(
             collective_id=0, has_side_effects=True, vmem_limit_bytes=60 * 2**20
@@ -474,7 +494,7 @@
         name="gather_verify",
     )(
         hidden,
-        norm_gain.reshape(1, depth),
+        norm_gain.reshape(depth // LANES, LANES),
         lm_head,
         draft_logits,
         draft_tokens.reshape(flat),

time: 124 us -> 106 us (0.85)
  Pallas kernels: 122 us -> 105 us
  local copies, waits for them, and re-layouts: 1.35 us -> 0 us
    pallas_call x1, Pallas kernels: 120 us -> 104 us  [body(): pl.pallas_call(main_kernel, out_shape=jax.ShapeDtypeStruct((5, *flat), jn...]
    reshape x1 -> x0, local copies, waits for them, and re-layouts: 1.35 us -> none  [body(): norm_gain.reshape(1, depth)]
where the time goes in v2:
time: 106 us
  Pallas kernels  105 us (99%)
    pallas_call x1, Pallas kernels, body(): pl.pallas_call(main_kernel, out_shape=jax.ShapeDtypeStruct((5, *flat), jn...  104 us

profile of v2, /device:TPU:0, one launch (start us, length us, event | category | flops | bytes accessed | tf_op | source)
XLA Modules:
  0.0 106.1 jit_solution(18269749025392557392)
XLA Ops:
  0.6 103.5 %gather_verify.1.stats_ref = f32[5,8,128]{2,1,0:T(8,128)} custom-call(bf16[16,7168]{1,0:T(8,128)(2,1)} %hidden_hbm.1, bf16[56,128]{1,0:T(8,128)(2,1)} %bitcast.12, bf16[7168,1024]{1,0:T(8,128)(2,1)} %head_hbm.1, bf16[1024,1024]{1,0:T(8,128)(2,1)} %draft_hbm.1, s32[8,128]{1,0:T(8,128)} %bitcast.15, s32[8,128]{1,0:T(8,128)} %bitcast.10), custom_call_target="tpu_custom_call" | custom-call | tf_op jit(solution)/shard_map/gather_verify/pallas_call | solution.py:463
  104.1 1.9 %tree.1 = (f32[8,128]{1,0:T(8,128)}, f32[8,128]{1,0:T(8,128)}, f32[8,128]{1,0:T(8,128)}, f32[8,128]{1,0:T(8,128)}, f32[8,128]{1,0:T(8,128)}) custom-call(f32[5,8,128]{2,1,0:T(8,128)} %gather_verify.1.stats_ref, s32[8,128]{1,0:T(8,128)} %bitcast.11, s32[8,128]{1,0:T(8,128)} %bitcast.13, f32[8,128]{1,0:T(8,128)} %bitcast.14), custom_call_target="tpu_custom_call" | custom-call | tf_op jit(solution)/shard_map/tree/pallas_call | solution.py:503

commit v3 on v2

--- a/solution.py
+++ b/solution.py
@@ -16,7 +16,7 @@
 MESH = pl.DeviceIdType.MESH
 
 ROUTES = ((0, 1, 2), (1, 2, 0), (2, 0, 1))
-GROUPS = ((2, 4, 4, 4, 4, 1), (2, 4, 4, 4, 4, 1), (2, 4, 4, 4, 3, 1))
+GROUPS = ((2, 5, 6, 4, 2), (2, 5, 6, 4, 2), (2, 5, 6, 3, 2))
 
 
 def relay_sides():
@@ -38,7 +38,6 @@
     + [(("join", axis), 0.3, 12.0 if axis else 0.0) for axis in range(4)]
     + [(("probs", b), 0.2, 0.0) for b in range(8)]
 )
-STRIPS = 2
 
 
 def plan():
@@ -72,21 +71,23 @@
                 if phase < 2:
                     send(now, p, g, phase + 1, 0)
                     send(now, p, g, phase + 1, 1)
-                else:
-                    ready.extend((p, g, n) for n in range(STRIPS))
+                if phase == 1:
+                    ready.append((p, g, 3))
+            if phase == 2:
+                ready.append((p, g, kind))
         elif draft and (due <= now or not ready):
             what, cost, _ = draft.pop(0)
             order.append(("draft", what))
             now = last = max(now, due) + cost
         else:
-            p, g, n = ready.pop(0)
-            order.append(("multiply", (p, g, n)))
-            now += 0.05 + 0.32 / STRIPS * max(2, GROUPS[p][g])
+            p, g, kind = ready.pop(0)
+            order.append(("multiply", (p, g, kind)))
+            now += 0.2 + 0.08 * max(2, GROUPS[p][g])
     return order
 
 
 ORDER = plan()
-PAIRS = [key[:2] for kind, key in ORDER if kind == "multiply" and key[2] == 0]
+PAIRS = [key[:2] for kind, key in ORDER if kind == "multiply" and key[2] == 3]
 MESSAGES = [m for kind, m in ORDER if kind == "take"]
 FIRST_TILE = {
     (p, g): sum(map(sum, GROUPS[:p])) + sum(GROUPS[p][:g]) for p in range(3) for g in range(len(GROUPS[p]))
@@ -108,8 +109,8 @@
     batch = lax.axis_index("batch")
     at = (me // 16, (me // 4) % 4, me % 4)
     stride = (16, 4, 1)
-    width = logits_ref.shape[1]
-    spans = logits_ref.shape[0] // LANES
+    width = weight_ref.shape[1]
+    spans = weight_ref.shape[0] // LANES
 
     def peer(axis, step):
         return (me + (lax.rem(at[axis] + step, SIDE) - at[axis]) * stride[axis], batch)
@@ -150,6 +151,8 @@
         part = hidden_ref[:, k * LANES : (k + 1) * LANES].astype(jnp.float32)
         gain = gain_ref[k : k + 1, :].astype(jnp.float32)
         rows_ref[k, at[0], at[1], at[2]] = (part * scale * gain).astype(jnp.bfloat16)
+    for y in range(SIDE):
+        logits_ref[y] = jnp.zeros(logits_ref.shape[1:], jnp.float32)
     pl.semaphore_wait(barrier, 9)
 
     number = {m: k for k, m in enumerate(MESSAGES)}
@@ -180,21 +183,22 @@
         copy.start()
         sent.append(copy)
 
-    def multiply(p, g, n):
+    def multiply(p, g, kind):
         first, many = FIRST_TILE[p, g], GROUPS[p][g]
-        if n == 0:
+        if kind == 3:
             head_copies[p, g].wait()
-        columns = slice(n * width // STRIPS, (n + 1) * width // STRIPS)
+        axis = ROUTES[p][2]
+        plane = [slice(None)] * 3
+        plane[axis] = lax.rem(at[axis] + (3, 1, 2, 0)[kind], SIDE)
+        count = SIDE * SIDE * hidden_ref.shape[0]
         left = jnp.concatenate(
-            [rows_ref[first + k].reshape(logits_ref.shape[0], LANES) for k in range(many)], axis=1
+            [rows_ref[(first + k, *plane)].reshape(count, LANES) for k in range(many)], axis=1
         )
         product = jnp.dot(
-            left, head_ref[first * LANES : (first + many) * LANES, columns], preferred_element_type=jnp.float32
+            left, head_ref[first * LANES : (first + many) * LANES, :], preferred_element_type=jnp.float32
         )
-        if (p, g) == PAIRS[0]:
-            logits_ref[:, columns] = product
-        else:
-            logits_ref[:, columns] += product
+        index = tuple(plane)
+        logits_ref[index] += product.reshape(SIDE, SIDE, hidden_ref.shape[0], width)
 
     def put(ref, stage, axis, values):
         for k, value in enumerate(values):
@@ -276,6 +280,10 @@
     def rows_of(b):
         return pl.ds(pl.multiple_of(b * LANES, LANES), LANES)
 
+    def logits_at(b, tile):
+        block = logits_ref[b // 2, pl.ds(lax.rem(b, 2) * 2, 2), :, :, tile]
+        return block.reshape(LANES, tile.stop - tile.start)
+
     def stat_row(k, b):
         return stat_ref[k, pl.ds(b, 1), :]
 
@@ -336,12 +344,12 @@
         rows = rows_of(b)
         top = jnp.full((LANES, LANES), -jnp.inf, jnp.float32)
         for tile in column_tiles():
-            top = jnp.maximum(top, logits_ref[rows, tile])
+            top = jnp.maximum(top, logits_at(b, tile))
         top = down(top, jnp.max)
         column = as_column(top)
         total = jnp.zeros((LANES, LANES), jnp.float32)
         for tile in column_tiles():
-            weight = jnp.exp(logits_ref[rows, tile] - column)
+            weight = jnp.exp(logits_at(b, tile) - column)
             weight_ref[rows, tile] = weight
             total += weight
         set_stat(3, b, top)
@@ -352,7 +360,7 @@
         rows = rows_of(b)
 
         def pieces(tile):
-            values = logits_ref[rows, tile]
+            values = logits_at(b, tile)
             high = values.astype(jnp.bfloat16)
             rest = values - high.astype(jnp.float32)
             middle = rest.astype(jnp.bfloat16)
@@ -473,7 +481,7 @@
             pltpu.VMEM(flat, jnp.int32),
             pltpu.VMEM(flat, jnp.int32),
             pltpu.VMEM((depth // LANES, SIDE, SIDE, SIDE, hidden.shape[0], LANES), jnp.bfloat16),
-            pltpu.VMEM((rows, width), jnp.float32),
+            pltpu.VMEM((SIDE, SIDE, SIDE, hidden.shape[0], width), jnp.float32),
             pltpu.VMEM((rows, width), jnp.float32),
             pltpu.VMEM((rows, width), jnp.float32),
             pltpu.VMEM((9, *flat), jnp.float32),

time: 106 us -> 94.9 us (0.90)
  Pallas kernels: 105 us -> 94.1 us
    pallas_call x1, Pallas kernels: 104 us -> 92.2 us  [body(): pl.pallas_call(main_kernel, out_shape=jax.ShapeDtypeStruct((5, *flat), jn...]
where the time goes in v3:
time: 94.9 us; the launch traced here: 94.8 us
  Pallas kernels  94.1 us (99%)
    pallas_call x1, Pallas kernels, body(): pl.pallas_call(main_kernel, out_shape=jax.ShapeDtypeStruct((5, *flat), jn...  92.2 us
    pallas_call x1, Pallas kernels, body(): pl.pallas_call(tree_kernel, out_shape=[jax.ShapeDtypeStruct(flat, jnp.flo...  1.92 us

profile of v3, /device:TPU:0, one launch (start us, length us, event | category | flops | bytes accessed | tf_op | source)
XLA Modules:
  0.0 94.8 jit_solution(15050429148389570859)
XLA Ops:
  0.6 92.2 %gather_verify.1.stats_ref = f32[5,8,128]{2,1,0:T(8,128)} custom-call(bf16[16,7168]{1,0:T(8,128)(2,1)} %hidden_hbm.1, bf16[56,128]{1,0:T(8,128)(2,1)} %bitcast.12, bf16[7168,1024]{1,0:T(8,128)(2,1)} %head_hbm.1, bf16[1024,1024]{1,0:T(8,128)(2,1)} %draft_hbm.1, s32[8,128]{1,0:T(8,128)} %bitcast.15, s32[8,128]{1,0:T(8,128)} %bitcast.10), custom_call_target="tpu_custom_call" | custom-call | tf_op jit(solution)/shard_map/gather_verify/pallas_call | solution.py:471
  92.8 1.9 %tree.1 = (f32[8,128]{1,0:T(8,128)}, f32[8,128]{1,0:T(8,128)}, f32[8,128]{1,0:T(8,128)}, f32[8,128]{1,0:T(8,128)}, f32[8,128]{1,0:T(8,128)}) custom-call(f32[5,8,128]{2,1,0:T(8,128)} %gather_verify.1.stats_ref, s32[8,128]{1,0:T(8,128)} %bitcast.11, s32[8,128]{1,0:T(8,128)} %bitcast.13, f32[8,128]{1,0:T(8,128)} %bitcast.14), custom_call_target="tpu_custom_call" | custom-call | tf_op jit(solution)/shard_map/tree/pallas_call | solution.py:511

commit v4 on v3

--- a/solution.py
+++ b/solution.py
@@ -16,13 +16,27 @@
 MESH = pl.DeviceIdType.MESH
 
 ROUTES = ((0, 1, 2), (1, 2, 0), (2, 0, 1))
-GROUPS = ((2, 5, 6, 4, 2), (2, 5, 6, 4, 2), (2, 5, 6, 3, 2))
+GROUPS = (
+    ((3, 7, 9), (3, 7, 9), (3, 7, 6, 3)),
+    ((3, 7, 9), (3, 7, 9), (3, 7, 6, 3)),
+    ((3, 6, 9), (3, 6, 9), (3, 6, 6, 3)),
+)
+
+
+def offset(p, phase, g):
+    return sum(sum(part[0]) for part in GROUPS[:p]) + sum(GROUPS[p][phase][:g])
+
+
+def finer(p, phase, g):
+    low = offset(p, phase, g)
+    high = low + GROUPS[p][phase][g]
+    return [k for k in range(len(GROUPS[p][phase + 1])) if low <= offset(p, phase + 1, k) < high]
 
 
 def relay_sides():
     sides = {}
-    for p, sizes in enumerate(GROUPS):
-        for phase in range(3):
+    for p, part in enumerate(GROUPS):
+        for phase, sizes in enumerate(part):
             lean = 0
             for g in sorted(range(len(sizes)), key=lambda g: -sizes[g]):
                 sides[p, g, phase] = 0 if lean <= 0 else 1
@@ -33,6 +47,15 @@
 SIDES = relay_sides()
 
 
+def kinds_sent(g, phase):
+    return (2, 0, 1) if phase == 0 or g == 0 and phase < 2 else (0, 1)
+
+
+def passed_on(message):
+    p, g, phase, kind = message
+    return kind == SIDES[p, g, phase] and 2 not in kinds_sent(g, phase)
+
+
 DRAFT = (
     [(("stats", b), 0.45, 2.0 if b == 0 else 0.0) for b in range(8)]
     + [(("join", axis), 0.3, 12.0 if axis else 0.0) for axis in range(4)]
@@ -41,22 +64,21 @@
 
 
 def plan():
-    rate, gap, latency = 44500.0, 0.2, 2.5
+    rate, gap, latency = 44500.0, 0.15, 2.2
     free = {(a, d): 0.0 for a in range(3) for d in range(2)}
     coming, count, have, order, ready = [], itertools.count(), set(), [], []
     draft = list(DRAFT)
 
     def send(now, p, g, phase, kind):
         way = (ROUTES[p][phase], kind if kind < 2 else SIDES[p, g, phase])
-        free[way] = max(now, free[way]) + gap + GROUPS[p][g] * 4096 * SIDE**phase / rate
+        free[way] = max(now, free[way]) + gap + GROUPS[p][phase][g] * 4096 * SIDE**phase / rate
         heapq.heappush(coming, (free[way] + latency, next(count), (p, g, phase, kind)))
 
     now, last = 0.0, 0.0
-    for g in range(max(map(len, GROUPS))):
+    for g in range(len(GROUPS[0][0])):
         for p in range(3):
-            if g < len(GROUPS[p]):
-                send(now, p, g, 0, 0)
-                send(now, p, g, 0, 1)
+            for kind in kinds_sent(g, 0):
+                send(now, p, g, 0, kind)
     while coming or ready or draft:
         due = last + draft[0][2] if draft else float("inf")
         if coming and coming[0][0] <= now or not ready and coming and coming[0][0] <= due:
@@ -65,14 +87,14 @@
             p, g, phase, kind = message
             have.add(message)
             order.append(("take", message))
-            if kind == SIDES[p, g, phase]:
+            if passed_on(message):
                 send(now, p, g, phase, 2)
             if all((p, g, phase, k) in have for k in range(3)):
-                if phase < 2:
-                    send(now, p, g, phase + 1, 0)
-                    send(now, p, g, phase + 1, 1)
-                if phase == 1:
-                    ready.append((p, g, 3))
+                for k in finer(p, phase, g) if phase < 2 else ():
+                    for way in kinds_sent(k, phase + 1):
+                        send(now, p, k, phase + 1, way)
+                    if phase == 1:
+                        ready.append((p, k, 3))
             if phase == 2:
                 ready.append((p, g, kind))
         elif draft and (due <= now or not ready):
@@ -82,16 +104,13 @@
         else:
             p, g, kind = ready.pop(0)
             order.append(("multiply", (p, g, kind)))
-            now += 0.2 + 0.08 * max(2, GROUPS[p][g])
+            now += 0.2 + 0.08 * max(2, GROUPS[p][2][g])
     return order
 
 
 ORDER = plan()
 PAIRS = [key[:2] for kind, key in ORDER if kind == "multiply" and key[2] == 3]
 MESSAGES = [m for kind, m in ORDER if kind == "take"]
-FIRST_TILE = {
-    (p, g): sum(map(sum, GROUPS[:p])) + sum(GROUPS[p][:g]) for p in range(3) for g in range(len(GROUPS[p]))
-}
 
 
 def as_column(row):
@@ -131,11 +150,11 @@
         copy.start()
     barrier = pltpu.get_barrier_semaphore()
     for axis in range(3):
-        for step in (1, 2, 3):
+        for step in (2, 1, 3):
             pl.semaphore_signal(barrier, inc=1, device_id=peer(axis, step), device_id_type=MESH)
     head_copies = {}
     for k, pair in enumerate(PAIRS):
-        span = pl.ds(FIRST_TILE[pair] * LANES, GROUPS[pair[0]][pair[1]] * LANES)
+        span = pl.ds(offset(pair[0], 2, pair[1]) * LANES, GROUPS[pair[0]][2][pair[1]] * LANES)
         head_copies[pair] = pltpu.make_async_copy(head_hbm.at[span], head_ref.at[span], head_sem.at[k])
         head_copies[pair].start()
 
@@ -162,8 +181,9 @@
         axis = ROUTES[p][phase]
         side = kind if kind < 2 else SIDES[p, g, phase]
         up = 1 if side == 0 else 3
-        begun = (SIDE - up) * (2 if kind == 2 else 1) if taking else ((SIDE - up) if kind == 2 else 0)
-        index = [pl.ds(FIRST_TILE[p, g], GROUPS[p][g]), *at]
+        routed = kind == 2 and 2 in kinds_sent(g, phase)
+        begun = (SIDE - up) * (2 if kind == 2 else 1) if taking else ((SIDE - up) if kind == 2 and not routed else 0)
+        index = [pl.ds(offset(p, phase, g), GROUPS[p][phase][g]), *at]
         for done in range(phase):
             index[1 + ROUTES[p][done]] = pl.ds(0, SIDE)
         index[1 + axis] = lax.rem(at[axis] + begun, SIDE)
@@ -174,7 +194,7 @@
             dst_ref=block,
             send_sem=send_sem.at[k],
             recv_sem=take_sem.at[k],
-            device_id=peer(axis, up),
+            device_id=peer(axis, 2 if routed else up),
             device_id_type=MESH,
         )
 
@@ -184,7 +204,7 @@
         sent.append(copy)
 
     def multiply(p, g, kind):
-        first, many = FIRST_TILE[p, g], GROUPS[p][g]
+        first, many = offset(p, 2, g), GROUPS[p][2][g]
         if kind == 3:
             head_copies[p, g].wait()
         axis = ROUTES[p][2]
@@ -243,12 +263,11 @@
         (o for o in itertools.product(range(SIDE), repeat=3) if any(o)), key=lambda o: -sum(min(v, SIDE - v) for v in o)
     )
 
+    places = [[lax.rem(at[axis] + step, SIDE) * stride[axis] for step in range(SIDE)] for axis in range(3)]
+
     def across(turn, k, back):
-        there = me
-        for axis in range(3):
-            step = shifts[k][axis]
-            here = lax.rem(at[axis] + (SIDE - step if back else step), SIDE)
-            there = there + (here - at[axis]) * stride[axis]
+        steps = [(SIDE - step) % SIDE if back else step for step in shifts[k]]
+        there = sum(places[axis][step] for axis, step in enumerate(steps))
         block = bank_ref.at[turn, there if back else me]
         return pltpu.make_async_remote_copy(
             src_ref=block,
@@ -403,11 +422,10 @@
                 out_ref[1] = stat_ref[6]
                 out_ref[4] = values[2]
 
-    for g in range(max(map(len, GROUPS))):
+    for g in range(len(GROUPS[0][0])):
         for p in range(3):
-            if g < len(GROUPS[p]):
-                send(p, g, 0, 0)
-                send(p, g, 0, 1)
+            for kind in kinds_sent(g, 0):
+                send(p, g, 0, kind)
     have = set()
     for kind, key in ORDER:
         if kind == "multiply":
@@ -418,20 +436,28 @@
             message(*key, True).wait_recv()
             p, g, phase, way = key
             have.add(key)
-            if way == SIDES[p, g, phase]:
+            if passed_on(key):
                 send(p, g, phase, 2)
             if phase < 2 and all((p, g, phase, k) in have for k in range(3)):
-                send(p, g, phase + 1, 0)
-                send(p, g, phase + 1, 1)
+                for k in finer(p, phase, g):
+                    for to in kinds_sent(k, phase + 1):
+                        send(p, k, phase + 1, to)
 
     over(target_stats, spans)
     cast(0, stat_ref[3] + jnp.log(stat_ref[4]))
     over(target_picks, 2)
     cast(1, stat_ref[5])
+    far = 2 * len(shifts)
+    for copy in sent[:-far]:
+        copy.wait_send()
+    del sent[:-far]
     target_lse = joined_lse(collected(0))
     stat_ref[7] = jnp.exp(stat_ref[3] - target_lse)
     over(residuals, spans)
     cast(2, stat_ref[8])
+    for copy in sent[:far]:
+        copy.wait_send()
+    del sent[:far]
     out_ref[0] = target_lse
     out_ref[3] = sum(collected(1))
     out_ref[2] = sum(collected(2))

time: 94.9 us -> 91.7 us (0.966)
  Pallas kernels: 94.1 us -> 90.9 us
    pallas_call x1, Pallas kernels: 92.2 us -> 88.9 us  [body(): pl.pallas_call(main_kernel, out_shape=jax.ShapeDtypeStruct((5, *flat), jn...]
where the time goes in v4:
time: 91.7 us; the launch traced here: 91.5 us
  Pallas kernels  90.9 us (99%)
    pallas_call x1, Pallas kernels, body(): pl.pallas_call(main_kernel, out_shape=jax.ShapeDtypeStruct((5, *flat), jn...  88.9 us
    pallas_call x1, Pallas kernels, body(): pl.pallas_call(tree_kernel, out_shape=[jax.ShapeDtypeStruct(flat, jnp.flo...  1.92 us

profile of v4, /device:TPU:0, one launch (start us, length us, event | category | flops | bytes accessed | tf_op | source)
XLA Modules:
  0.0 91.5 jit_solution(14035721147021440344)
XLA Ops:
  0.6 88.9 %gather_verify.1.stats_ref = f32[5,8,128]{2,1,0:T(8,128)} custom-call(bf16[16,7168]{1,0:T(8,128)(2,1)} %hidden_hbm.1, bf16[56,128]{1,0:T(8,128)(2,1)} %bitcast.12, bf16[7168,1024]{1,0:T(8,128)(2,1)} %head_hbm.1, bf16[1024,1024]{1,0:T(8,128)(2,1)} %draft_hbm.1, s32[8,128]{1,0:T(8,128)} %bitcast.15, s32[8,128]{1,0:T(8,128)} %bitcast.10), custom_call_target="tpu_custom_call" | custom-call | tf_op jit(solution)/shard_map/gather_verify/pallas_call | solution.py:497
  89.6 1.9 %tree.1 = (f32[8,128]{1,0:T(8,128)}, f32[8,128]{1,0:T(8,128)}, f32[8,128]{1,0:T(8,128)}, f32[8,128]{1,0:T(8,128)}, f32[8,128]{1,0:T(8,128)}) custom-call(f32[5,8,128]{2,1,0:T(8,128)} %gather_verify.1.stats_ref, s32[8,128]{1,0:T(8,128)} %bitcast.11, s32[8,128]{1,0:T(8,128)} %bitcast.13, f32[8,128]{1,0:T(8,128)} %bitcast.14), custom_call_target="tpu_custom_call" | custom-call | tf_op jit(solution)/shard_map/tree/pallas_call | solution.py:537

commit v5 on v4

--- a/solution.py
+++ b/solution.py
@@ -17,9 +17,9 @@
 
 ROUTES = ((0, 1, 2), (1, 2, 0), (2, 0, 1))
 GROUPS = (
-    ((3, 7, 9), (3, 7, 9), (3, 7, 6, 3)),
-    ((3, 7, 9), (3, 7, 9), (3, 7, 6, 3)),
-    ((3, 6, 9), (3, 6, 9), (3, 6, 6, 3)),
+    ((3, 6, 10), (3, 6, 10), (3, 6, 5, 3, 2)),
+    ((3, 6, 10), (3, 6, 10), (3, 6, 5, 3, 2)),
+    ((3, 6, 9), (3, 6, 9), (3, 6, 4, 3, 2)),
 )
 
 
@@ -121,7 +121,7 @@
     hidden_hbm, gain_hbm, head_hbm, draft_hbm, tokens_hbm, parents_hbm,
     out_ref,
     hidden_ref, gain_ref, head_ref, draft_ref, tokens_ref, parents_ref,
-    rows_ref, logits_ref, weight_ref, draft_prob_ref, stat_ref, pair_ref, bank_ref,
+    rows_ref, logits_ref, weight_ref, draft_prob_ref, stat_ref, pair_ref, pick_ref, bank_ref,
     small_sem, head_sem, send_sem, take_sem, swap_send_sem, swap_take_sem, far_send_sem, far_take_sem,
 ):
     me = lax.axis_index("vocab")
@@ -446,21 +446,31 @@
     over(target_stats, spans)
     cast(0, stat_ref[3] + jnp.log(stat_ref[4]))
     over(target_picks, 2)
-    cast(1, stat_ref[5])
-    far = 2 * len(shifts)
-    for copy in sent[:-far]:
+    def pick_sum(stage):
+        taken(pick_ref, stage, 3 + stage, stage)
+        return sum(pick_ref[stage, c, 0] for c in range(SIDE))
+
+    put(pick_ref, 0, 0, (stat_ref[5],))
+    swap(pick_ref, 0, 3, 0)
+    early = len(sent) - len(shifts) - 3
+    for copy in sent[:early]:
         copy.wait_send()
-    del sent[:-far]
+    del sent[:early]
+    put(pick_ref, 1, 1, (pick_sum(0),))
+    swap(pick_ref, 1, 4, 1)
     target_lse = joined_lse(collected(0))
     stat_ref[7] = jnp.exp(stat_ref[3] - target_lse)
     over(residuals, spans)
-    cast(2, stat_ref[8])
-    for copy in sent[:far]:
+    cast(1, stat_ref[8])
+    out_ref[0] = target_lse
+    early = len(sent) - len(shifts)
+    for copy in sent[:early]:
         copy.wait_send()
-    del sent[:far]
-    out_ref[0] = target_lse
-    out_ref[3] = sum(collected(1))
-    out_ref[2] = sum(collected(2))
+    del sent[:early]
+    put(pick_ref, 2, 2, (pick_sum(1),))
+    swap(pick_ref, 2, 5, 2)
+    out_ref[3] = pick_sum(2)
+    out_ref[2] = sum(collected(1))
     for copy in sent:
         copy.wait_send()
 
@@ -512,15 +522,16 @@
             pltpu.VMEM((rows, width), jnp.float32),
             pltpu.VMEM((9, *flat), jnp.float32),
             pltpu.VMEM((3, SIDE, 3, *flat), jnp.float32),
-            pltpu.VMEM((3, SIDE**3, *flat), jnp.float32),
+            pltpu.VMEM((3, SIDE, 1, *flat), jnp.float32),
+            pltpu.VMEM((2, SIDE**3, *flat), jnp.float32),
             pltpu.SemaphoreType.DMA((5,)),
             pltpu.SemaphoreType.DMA((len(PAIRS),)),
             pltpu.SemaphoreType.DMA((len(MESSAGES),)),
             pltpu.SemaphoreType.DMA((len(MESSAGES),)),
-            pltpu.SemaphoreType.DMA((3, 3)),
-            pltpu.SemaphoreType.DMA((3, 3)),
-            pltpu.SemaphoreType.DMA((3, SIDE**3 - 1)),
-            pltpu.SemaphoreType.DMA((3, SIDE**3 - 1)),
+            pltpu.SemaphoreType.DMA((6, 3)),
+            pltpu.SemaphoreType.DMA((6, 3)),
+            pltpu.SemaphoreType.DMA((2, SIDE**3 - 1)),
+            pltpu.SemaphoreType.DMA((2, SIDE**3 - 1)),
         ],
         compiler_params=pltpu.CompilerParams(
             collective_id=0, has_side_effects=True, vmem_limit_bytes=60 * 2**20

time: 91.7 us -> 89.7 us (0.978)
  Pallas kernels: 90.9 us -> 88.9 us
    pallas_call x1, Pallas kernels: 88.9 us -> 87 us  [body(): pl.pallas_call(main_kernel, out_shape=jax.ShapeDtypeStruct((5, *flat), jn...]
where the time goes in v5:
time: 89.7 us; the launch traced here: 89.6 us
  Pallas kernels  88.9 us (99%)
    pallas_call x1, Pallas kernels, body(): pl.pallas_call(main_kernel, out_shape=jax.ShapeDtypeStruct((5, *flat), jn...  87 us
    pallas_call x1, Pallas kernels, body(): pl.pallas_call(tree_kernel, out_shape=[jax.ShapeDtypeStruct(flat, jnp.flo...  1.92 us

profile of v5, /device:TPU:0, one launch (start us, length us, event | category | flops | bytes accessed | tf_op | source)
XLA Modules:
  0.0 89.6 jit_solution(9617731224253821842)
XLA Ops:
  0.6 87.0 %gather_verify.1.stats_ref = f32[5,8,128]{2,1,0:T(8,128)} custom-call(bf16[16,7168]{1,0:T(8,128)(2,1)} %hidden_hbm.1, bf16[56,128]{1,0:T(8,128)(2,1)} %bitcast.12, bf16[7168,1024]{1,0:T(8,128)(2,1)} %head_hbm.1, bf16[1024,1024]{1,0:T(8,128)(2,1)} %draft_hbm.1, s32[8,128]{1,0:T(8,128)} %bitcast.15, s32[8,128]{1,0:T(8,128)} %bitcast.10), custom_call_target="tpu_custom_call" | custom-call | tf_op jit(solution)/shard_map/gather_verify/pallas_call | solution.py:507
  87.6 1.9 %tree.1 = (f32[8,128]{1,0:T(8,128)}, f32[8,128]{1,0:T(8,128)}, f32[8,128]{1,0:T(8,128)}, f32[8,128]{1,0:T(8,128)}, f32[8,128]{1,0:T(8,128)}) custom-call(f32[5,8,128]{2,1,0:T(8,128)} %gather_verify.1.stats_ref, s32[8,128]{1,0:T(8,128)} %bitcast.11, s32[8,128]{1,0:T(8,128)} %bitcast.13, f32[8,128]{1,0:T(8,128)} %bitcast.14), custom_call_target="tpu_custom_call" | custom-call | tf_op jit(solution)/shard_map/tree/pallas_call | solution.py:548

commit v6 on v5

--- a/solution.py
+++ b/solution.py
@@ -456,14 +456,14 @@
     for copy in sent[:early]:
         copy.wait_send()
     del sent[:early]
-    put(pick_ref, 1, 1, (pick_sum(0),))
-    swap(pick_ref, 1, 4, 1)
     target_lse = joined_lse(collected(0))
     stat_ref[7] = jnp.exp(stat_ref[3] - target_lse)
     over(residuals, spans)
     cast(1, stat_ref[8])
     out_ref[0] = target_lse
-    early = len(sent) - len(shifts)
+    put(pick_ref, 1, 1, (pick_sum(0),))
+    swap(pick_ref, 1, 4, 1)
+    early = len(sent) - len(shifts) - 3
     for copy in sent[:early]:
         copy.wait_send()
     del sent[:early]

time: 89.7 us -> 90.2 us (level)
  no operation moved by 1% of the time
where the time goes in v6:
time: 90.2 us; the launch traced here: 90.1 us
  Pallas kernels  89.4 us (99%)
    pallas_call x1, Pallas kernels, body(): pl.pallas_call(main_kernel, out_shape=jax.ShapeDtypeStruct((5, *flat), jn...  87.5 us
    pallas_call x1, Pallas kernels, body(): pl.pallas_call(tree_kernel, out_shape=[jax.ShapeDtypeStruct(flat, jnp.flo...  1.92 us

profile of v6, /device:TPU:0, one launch (start us, length us, event | category | flops | bytes accessed | tf_op | source)
XLA Modules:
  0.0 90.1 jit_solution(6999081581961819068)
XLA Ops:
  0.6 87.5 %gather_verify.1.stats_ref = f32[5,8,128]{2,1,0:T(8,128)} custom-call(bf16[16,7168]{1,0:T(8,128)(2,1)} %hidden_hbm.1, bf16[56,128]{1,0:T(8,128)(2,1)} %bitcast.12, bf16[7168,1024]{1,0:T(8,128)(2,1)} %head_hbm.1, bf16[1024,1024]{1,0:T(8,128)(2,1)} %draft_hbm.1, s32[8,128]{1,0:T(8,128)} %bitcast.15, s32[8,128]{1,0:T(8,128)} %bitcast.10), custom_call_target="tpu_custom_call" | custom-call | tf_op jit(solution)/shard_map/gather_verify/pallas_call | solution.py:507
  88.1 1.9 %tree.1 = (f32[8,128]{1,0:T(8,128)}, f32[8,128]{1,0:T(8,128)}, f32[8,128]{1,0:T(8,128)}, f32[8,128]{1,0:T(8,128)}, f32[8,128]{1,0:T(8,128)}) custom-call(f32[5,8,128]{2,1,0:T(8,128)} %gather_verify.1.stats_ref, s32[8,128]{1,0:T(8,128)} %bitcast.11, s32[8,128]{1,0:T(8,128)} %bitcast.13, f32[8,128]{1,0:T(8,128)} %bitcast.14), custom_call_target="tpu_custom_call" | custom-call | tf_op jit(solution)/shard_map/tree/pallas_call | solution.py:548
